TPU v7x, 512 devices: a whole 4x4x16 slice. The times are simulated.
512 devices in a mesh: dp: 16 (over y_lo, x, core), ctx: 32 (over y_hi, z).
Axes of the slice: x: 4, y: 4 (y_hi: 2, y_lo: 2; y = y_hi * 2 + y_lo), z: 16, core: 2. Of those that a mesh axis runs over, the one named last changes fastest.
Arguments:
- grad_out: bfloat16 [65536, 4096], P(('dp', 'ctx')), may hold values from -24 to 24
- gate: bfloat16 [65536, 4096], P(('dp', 'ctx')), may hold values from -6 to 6
- conv_in: bfloat16 [65536, 4096], P(('dp', 'ctx')), may hold values from -6 to 6
- filt: bfloat16 [4096, 64], P('dp'), may hold values from -0.75 to 0.75
- doc_end: int32 [65536], P(('dp', 'ctx')), may hold values from 1 to 65536, as said below
Outputs:
- grad_in: bfloat16 [65536, 4096], P(('dp', 'ctx'))
- grad_filt: float32 [4096, 64], P('dp')
Inputs may be any that keep to these rules, and one draw needn't show every extreme that they name: doc_end is the same for all rows of one document and larger than the row's own index; no document crosses a multiple of 4096.
All inputs are finite; a program needn't handle non-finite values.
Results may differ from a plain program's by a relative error of at most 0.0049.
Values may be sent and summed in bfloat16 or wider, within the bound.
A program may use at most 64 MiB of HBM per device.

v0:
```python
import jax
import jax.numpy as jnp
from jax import lax
from jax.sharding import PartitionSpec as P


def from_behind(value, axis, steps):
    count = lax.axis_size(axis)
    first, last = (max(0, -steps), min(count, count - steps))
    return lax.ppermute(value, axis, [(source, source + steps) for source in range(first, last)])


def body(grad_out, gate, conv_in, filt, doc_end):
    row_count, channels = grad_out.shape
    tap_count = filt.shape[1]
    group_size = 8
    whole_filter = lax.all_gather(filt, "dp", axis=0, tiled=True)
    filter_rows = whole_filter.T
    grad_y = (grad_out.astype(jnp.float32) * gate.astype(jnp.float32)).astype(jnp.bfloat16)
    following = from_behind(grad_y, "ctx", -1)
    extended = jnp.concatenate([grad_y, following], axis=0)
    first_row = (lax.axis_index("dp") * lax.axis_size("ctx") + lax.axis_index("ctx")) * row_count
    remaining = doc_end - (first_row + jnp.arange(row_count, dtype=jnp.int32))
    within = jnp.arange(group_size, dtype=jnp.int32)

    def one_group(which, state):
        accum, tap_rows = state
        base = (which * group_size).astype(jnp.int32)
        offsets = base + within
        windows = jax.vmap(lambda offset: lax.dynamic_slice_in_dim(extended, offset, row_count, 0))(
            offsets
        )
        inside = (offsets[:, None] < remaining[None, :])[:, :, None]
        windows = jnp.where(inside, windows, jnp.zeros((), jnp.bfloat16))
        weights = lax.dynamic_slice_in_dim(filter_rows, base, group_size, 0)
        accum = accum + jnp.einsum(
            "trc,tc->rc", windows, weights, preferred_element_type=jnp.float32
        )
        tap_block = jnp.einsum("trc,rc->tc", windows, conv_in, preferred_element_type=jnp.float32)
        tap_rows = lax.dynamic_update_slice_in_dim(tap_rows, tap_block, base, 0)
        return (accum, tap_rows)

    start = (
        jnp.zeros((row_count, channels), jnp.float32),
        jnp.zeros((tap_count, channels), jnp.float32),
    )
    accum, tap_rows = lax.fori_loop(0, tap_count // group_size, one_group, start)
    grad_in = accum.astype(jnp.bfloat16)
    filt_terms = tap_rows.T
    owned = lax.psum_scatter(filt_terms, "dp", scatter_dimension=0, tiled=True)
    grad_filt = lax.psum(owned, "ctx")
    return (grad_in, grad_filt)


def solution(mesh):
    placed = (
        P(("dp", "ctx"), None),
        P(("dp", "ctx"), None),
        P(("dp", "ctx"), None),
        P("dp", None),
        P(("dp", "ctx")),
    )
    return jax.shard_map(
        body,
        mesh=mesh,
        in_specs=placed,
        out_specs=(P(("dp", "ctx"), None), P("dp", None)),
        check_vma=False,
    )
```

profile of v0, /device:TPU:2, one launch (start us, length us, event | category | flops | bytes accessed | tf_op | source)
XLA Modules:
  0.0 696.5 jit_solution(7880382249761035540)
XLA Ops:
  7.2 1.9 multiply_convert_fusion
  11.1 24.8 %all_gather.3 = bf16[4096,64]{0,1:T(8,128)(2,1)} all-gather(bf16[256,64]{0,1:T(8,128)(2,1)} %param.10), channel_id=1, replica_groups=mesh['dp'=16,'ctx'=32] {'dp'}, dimensions={0}, use_global_device_ids=true | all-gather | bytes 557056 | tf_op jit(solution)/shard_map/all_gather | solution.py:17
  39.0 302.4 %while.23 = (s32[]{:T(128)}, f32[128,4096]{1,0:T(8,128)}, f32[64,4096]{1,0:T(8,128)}, bf16[64,4096]{1,0:T(8,128)(2,1)}, s32[128]{0:T(128)S(1)}, /*index=5*/bf16[...) while((s32[]{:T(128)}, f32[128,4096]{1,0:T(8,128)}, ...), condition=%wide.region_1.2_spmd.clone.clone, body=%wide.region_0.1_spmd.clone.sunk.clone | while | flops 34604080 | bytes 66786340 | solution.py:47
  39.9 19.0 %while.22 = (s32[]{:T(128)}, bf16[256,4096]{1,0:T(8,128)(2,1)S(1)}, s32[8,2]{0,1:T(2,128)S(1)}, bf16[8,128,4096]{2,1,0:T(8,128)(2,1)}, s32[]{:T(128)}) while((s32[]{:T(128)}, bf16[256,4096]{1,0:T(8,128)(2,1)S(1)}, s32[8,2]{0,1:T(2,128)S(1)}, bf16[8,128,4096]{2,1,0:T(8,128)(2,1)}, s32[]{:T(128)}) %tuple.56), condition=%wide.while_cond, body=%wide.while_body.sunk | while | flops 2 | bytes 2098265 | solution.py:30
  42.8 1.8 bitcast_dynamic-update-slice_fusion.5
  59.0 8.2 %multiply_reduce_fusion.6 = f32[4096,128]{0,1:T(8,128)} fusion(f32[4096,8]{0,1:T(8,128)S(1)} %bitcast_convert_fusion.6, bf16[8,128,4096]{2,1,0:T(8,128)(2,1)} %get-tuple-element.289, pred[8,128]{1,0:T(8,128)(4,1)S(1)} %broadcast_compare_fusion.3), kind=kLoop, calls=%fused_computation.4.clone.1.clone | loop fusion | flops 16252928 | bytes 10617856 | tf_op jit(solution)/shard_map/while/body/eval_jaxpr/trc,tc->rc/dot_general | solution.py:36
  67.1 3.4 bitcast_add_fusion.3
  71.9 3.7 multiply_reduce_fusion.7
  77.1 19.0 %while.22 = (s32[]{:T(128)}, bf16[256,4096]{1,0:T(8,128)(2,1)S(1)}, s32[8,2]{0,1:T(2,128)S(1)}, bf16[8,128,4096]{2,1,0:T(8,128)(2,1)}, s32[]{:T(128)}) while((s32[]{:T(128)}, bf16[256,4096]{1,0:T(8,128)(2,1)S(1)}, s32[8,2]{0,1:T(2,128)S(1)}, bf16[8,128,4096]{2,1,0:T(8,128)(2,1)}, s32[]{:T(128)}) %tuple.56), condition=%wide.while_cond, body=%wide.while_body.sunk | while | flops 2 | bytes 2098265 | solution.py:30
  80.1 1.8 bitcast_dynamic-update-slice_fusion.5
  96.2 8.2 %multiply_reduce_fusion.6 = f32[4096,128]{0,1:T(8,128)} fusion(f32[4096,8]{0,1:T(8,128)S(1)} %bitcast_convert_fusion.6, bf16[8,128,4096]{2,1,0:T(8,128)(2,1)} %get-tuple-element.289, pred[8,128]{1,0:T(8,128)(4,1)S(1)} %broadcast_compare_fusion.3), kind=kLoop, calls=%fused_computation.4.clone.1.clone | loop fusion | flops 16252928 | bytes 10617856 | tf_op jit(solution)/shard_map/while/body/eval_jaxpr/trc,tc->rc/dot_general | solution.py:36
  104.4 4.0 bitcast_add_fusion.3
  109.8 3.7 multiply_reduce_fusion.7
  115.0 19.0 %while.22 = (s32[]{:T(128)}, bf16[256,4096]{1,0:T(8,128)(2,1)S(1)}, s32[8,2]{0,1:T(2,128)S(1)}, bf16[8,128,4096]{2,1,0:T(8,128)(2,1)}, s32[]{:T(128)}) while((s32[]{:T(128)}, bf16[256,4096]{1,0:T(8,128)(2,1)S(1)}, s32[8,2]{0,1:T(2,128)S(1)}, bf16[8,128,4096]{2,1,0:T(8,128)(2,1)}, s32[]{:T(128)}) %tuple.56), condition=%wide.while_cond, body=%wide.while_body.sunk | while | flops 2 | bytes 2098265 | solution.py:30
  118.0 1.8 bitcast_dynamic-update-slice_fusion.5
  134.1 8.2 %multiply_reduce_fusion.6 = f32[4096,128]{0,1:T(8,128)} fusion(f32[4096,8]{0,1:T(8,128)S(1)} %bitcast_convert_fusion.6, bf16[8,128,4096]{2,1,0:T(8,128)(2,1)} %get-tuple-element.289, pred[8,128]{1,0:T(8,128)(4,1)S(1)} %broadcast_compare_fusion.3), kind=kLoop, calls=%fused_computation.4.clone.1.clone | loop fusion | flops 16252928 | bytes 10617856 | tf_op jit(solution)/shard_map/while/body/eval_jaxpr/trc,tc->rc/dot_general | solution.py:36
  142.2 4.0 bitcast_add_fusion.3
  147.6 3.7 multiply_reduce_fusion.7
  152.9 19.0 %while.22 = (s32[]{:T(128)}, bf16[256,4096]{1,0:T(8,128)(2,1)S(1)}, s32[8,2]{0,1:T(2,128)S(1)}, bf16[8,128,4096]{2,1,0:T(8,128)(2,1)}, s32[]{:T(128)}) while((s32[]{:T(128)}, bf16[256,4096]{1,0:T(8,128)(2,1)S(1)}, s32[8,2]{0,1:T(2,128)S(1)}, bf16[8,128,4096]{2,1,0:T(8,128)(2,1)}, s32[]{:T(128)}) %tuple.56), condition=%wide.while_cond, body=%wide.while_body.sunk | while | flops 2 | bytes 2098265 | solution.py:30
  155.8 1.8 bitcast_dynamic-update-slice_fusion.5
  165.3 1.8 bitcast_dynamic-update-slice_fusion.5
  172.0 8.2 %multiply_reduce_fusion.6 = f32[4096,128]{0,1:T(8,128)} fusion(f32[4096,8]{0,1:T(8,128)S(1)} %bitcast_convert_fusion.6, bf16[8,128,4096]{2,1,0:T(8,128)(2,1)} %get-tuple-element.289, pred[8,128]{1,0:T(8,128)(4,1)S(1)} %broadcast_compare_fusion.3), kind=kLoop, calls=%fused_computation.4.clone.1.clone | loop fusion | flops 16252928 | bytes 10617856 | tf_op jit(solution)/shard_map/while/body/eval_jaxpr/trc,tc->rc/dot_general | solution.py:36
  180.1 4.0 bitcast_add_fusion.3
  185.5 3.7 multiply_reduce_fusion.7
  190.8 19.0 %while.22 = (s32[]{:T(128)}, bf16[256,4096]{1,0:T(8,128)(2,1)S(1)}, s32[8,2]{0,1:T(2,128)S(1)}, bf16[8,128,4096]{2,1,0:T(8,128)(2,1)}, s32[]{:T(128)}) while((s32[]{:T(128)}, bf16[256,4096]{1,0:T(8,128)(2,1)S(1)}, s32[8,2]{0,1:T(2,128)S(1)}, bf16[8,128,4096]{2,1,0:T(8,128)(2,1)}, s32[]{:T(128)}) %tuple.56), condition=%wide.while_cond, body=%wide.while_body.sunk | while | flops 2 | bytes 2098265 | solution.py:30
  193.7 1.8 bitcast_dynamic-update-slice_fusion.5
  203.2 1.8 bitcast_dynamic-update-slice_fusion.5
  209.8 8.2 %multiply_reduce_fusion.6 = f32[4096,128]{0,1:T(8,128)} fusion(f32[4096,8]{0,1:T(8,128)S(1)} %bitcast_convert_fusion.6, bf16[8,128,4096]{2,1,0:T(8,128)(2,1)} %get-tuple-element.289, pred[8,128]{1,0:T(8,128)(4,1)S(1)} %broadcast_compare_fusion.3), kind=kLoop, calls=%fused_computation.4.clone.1.clone | loop fusion | flops 16252928 | bytes 10617856 | tf_op jit(solution)/shard_map/while/body/eval_jaxpr/trc,tc->rc/dot_general | solution.py:36
  218.0 4.0 bitcast_add_fusion.3
  223.4 3.7 multiply_reduce_fusion.7
  228.7 19.0 %while.22 = (s32[]{:T(128)}, bf16[256,4096]{1,0:T(8,128)(2,1)S(1)}, s32[8,2]{0,1:T(2,128)S(1)}, bf16[8,128,4096]{2,1,0:T(8,128)(2,1)}, s32[]{:T(128)}) while((s32[]{:T(128)}, bf16[256,4096]{1,0:T(8,128)(2,1)S(1)}, s32[8,2]{0,1:T(2,128)S(1)}, bf16[8,128,4096]{2,1,0:T(8,128)(2,1)}, s32[]{:T(128)}) %tuple.56), condition=%wide.while_cond, body=%wide.while_body.sunk | while | flops 2 | bytes 2098265 | solution.py:30
  231.6 1.8 bitcast_dynamic-update-slice_fusion.5
  247.7 8.2 %multiply_reduce_fusion.6 = f32[4096,128]{0,1:T(8,128)} fusion(f32[4096,8]{0,1:T(8,128)S(1)} %bitcast_convert_fusion.6, bf16[8,128,4096]{2,1,0:T(8,128)(2,1)} %get-tuple-element.289, pred[8,128]{1,0:T(8,128)(4,1)S(1)} %broadcast_compare_fusion.3), kind=kLoop, calls=%fused_computation.4.clone.1.clone | loop fusion | flops 16252928 | bytes 10617856 | tf_op jit(solution)/shard_map/while/body/eval_jaxpr/trc,tc->rc/dot_general | solution.py:36
  255.9 4.0 bitcast_add_fusion.3
  261.3 3.7 multiply_reduce_fusion.7
  266.5 19.0 %while.22 = (s32[]{:T(128)}, bf16[256,4096]{1,0:T(8,128)(2,1)S(1)}, s32[8,2]{0,1:T(2,128)S(1)}, bf16[8,128,4096]{2,1,0:T(8,128)(2,1)}, s32[]{:T(128)}) while((s32[]{:T(128)}, bf16[256,4096]{1,0:T(8,128)(2,1)S(1)}, s32[8,2]{0,1:T(2,128)S(1)}, bf16[8,128,4096]{2,1,0:T(8,128)(2,1)}, s32[]{:T(128)}) %tuple.56), condition=%wide.while_cond, body=%wide.while_body.sunk | while | flops 2 | bytes 2098265 | solution.py:30
  269.5 1.8 bitcast_dynamic-update-slice_fusion.5
  285.6 8.2 %multiply_reduce_fusion.6 = f32[4096,128]{0,1:T(8,128)} fusion(f32[4096,8]{0,1:T(8,128)S(1)} %bitcast_convert_fusion.6, bf16[8,128,4096]{2,1,0:T(8,128)(2,1)} %get-tuple-element.289, pred[8,128]{1,0:T(8,128)(4,1)S(1)} %broadcast_compare_fusion.3), kind=kLoop, calls=%fused_computation.4.clone.1.clone | loop fusion | flops 16252928 | bytes 10617856 | tf_op jit(solution)/shard_map/while/body/eval_jaxpr/trc,tc->rc/dot_general | solution.py:36
  293.7 4.0 bitcast_add_fusion.3
  299.1 3.7 multiply_reduce_fusion.7
  304.4 19.0 %while.22 = (s32[]{:T(128)}, bf16[256,4096]{1,0:T(8,128)(2,1)S(1)}, s32[8,2]{0,1:T(2,128)S(1)}, bf16[8,128,4096]{2,1,0:T(8,128)(2,1)}, s32[]{:T(128)}) while((s32[]{:T(128)}, bf16[256,4096]{1,0:T(8,128)(2,1)S(1)}, s32[8,2]{0,1:T(2,128)S(1)}, bf16[8,128,4096]{2,1,0:T(8,128)(2,1)}, s32[]{:T(128)}) %tuple.56), condition=%wide.while_cond, body=%wide.while_body.sunk | while | flops 2 | bytes 2098265 | solution.py:30
  307.3 1.8 bitcast_dynamic-update-slice_fusion.5
  323.5 8.2 %multiply_reduce_fusion.6 = f32[4096,128]{0,1:T(8,128)} fusion(f32[4096,8]{0,1:T(8,128)S(1)} %bitcast_convert_fusion.6, bf16[8,128,4096]{2,1,0:T(8,128)(2,1)} %get-tuple-element.289, pred[8,128]{1,0:T(8,128)(4,1)S(1)} %broadcast_compare_fusion.3), kind=kLoop, calls=%fused_computation.4.clone.1.clone | loop fusion | flops 16252928 | bytes 10617856 | tf_op jit(solution)/shard_map/while/body/eval_jaxpr/trc,tc->rc/dot_general | solution.py:36
  331.6 4.0 bitcast_add_fusion.3
  337.0 3.7 multiply_reduce_fusion.7
  341.5 70.3 %reduce-scatter.2.cloned.1.call-done = f32[256,64]{0,1:T(8,128)} async-done(((f32[4096,64]{0,1:T(8,128)}), f32[256,64]{0,1:T(8,128)}) %reduce-scatter.2.cloned.1.call-update) | async-done | bytes 65552 | tf_op jit(solution)/shard_map/reduce_scatter | solution.py:50
  411.8 2.7 convert_element_type.15
  414.5 273.6 %all-reduce.3.cloned.1.call-done = f32[256,64]{0,1:T(8,128)} async-done(((f32[256,64]{0,1:T(8,128)}), f32[256,64]{0,1:T(8,128)}) %all-reduce.3.cloned.1.call-update) | async-done | bytes 65552 | tf_op jit(solution)/shard_map/psum | solution.py:51
  (277 shorter events, 163.7 us)
Async XLA Ops:
  7.2 31.8 %copy-start.1 = (bf16[128,4096]{1,0:T(8,128)(2,1)S(1)}, bf16[128,4096]{1,0:T(8,128)(2,1)}, u32[]{:S(2)}) copy-start(bf16[128,4096]{1,0:T(8,128)(2,1)} %param.9) | copy-start | bytes 3145732
  7.2 404.6 %reduce-scatter.2.cloned.1.call-start = ((), (), s32[]{:S(2)}) async-start(), calls=%async_computation.1 | async-start | bytes 1114112 | tf_op jit(solution)/shard_map/reduce_scatter | solution.py:50
  9.1 26.8 %copy-start.2 = (bf16[128,4096]{1,0:T(8,128)(2,1)}, bf16[128,4096]{1,0:T(8,128)(2,1)S(1)}, u32[]{:S(2)}) copy-start(bf16[128,4096]{1,0:T(8,128)(2,1)S(1)} %multiply_convert_fusion) | copy-start | bytes 3145732
  9.1 27.1 %collective-permute-start = (bf16[128,4096]{1,0:T(8,128)(2,1)S(1)}, bf16[128,4096]{1,0:T(8,128)(2,1)}, u32[]{:S(2)}, u32[]{:S(2)}) collective-permute-start(bf16[128,4096]{1,0:T(8,128)(2,1)S(1)} %multiply_convert_fusion), channel_id=1, source_target_pairs={{1,0},{2,1},{3,2},{4,3},{5,4},{6,5},{7,6},{8,7},{9,8},{10,9},{11,1... | collective-permute-start | bytes 3145736 | tf_op jit(solution)/shard_map/ppermute | solution.py:10
  67.1 4.8 copy-start
  104.4 5.4 copy-start
  142.2 5.4 copy-start
  180.1 5.4 copy-start
  218.0 5.4 copy-start
  255.9 5.4 copy-start
  293.7 5.4 copy-start
  331.6 5.4 copy-start
  341.4 346.7 %all-reduce.3.cloned.1.call-start = ((), (), s32[]{:S(2)}) async-start(), calls=%async_computation.2 | async-start | bytes 131072 | tf_op jit(solution)/shard_map/psum | solution.py:51
Sparse Core Ops, SparseCore 0:
  341.6 70.2 reduce-scatter.1
  414.7 273.3 all-reduce.2
where the time goes:
time: 698 us; the launch traced here: 696 us
  waiting for transfers between devices  344 us (49%)
  local copies, waits for them, and re-layouts  169 us (24%)
  other arithmetic  142 us (20%)
  blocking collectives  24.8 us (4%)
  between operations  14.1 us (2%)
    psum x1, waiting for transfers between devices, body(): grad_filt = lax.psum(owned, 'ctx')  274 us
    gather x192, local copies, waits for them, and re-layouts  152 us
    reduce_scatter x1, waiting for transfers between devices, body(): owned = lax.psum_scatter(filt_terms, 'dp', scatter_dimension=0, tiled=True)  70.3 us
    dot_general x8, other arithmetic, one_group(): jnp.einsum('trc,tc->rc', windows, weights, preferred_element_type=jnp.flo...  65.2 us
    add x8, other arithmetic, one_group(): accum + jnp.einsum('trc,tc->rc', windows, weights, preferred_element_type...  31.5 us
    dot_general x8, other arithmetic, one_group(): jnp.einsum('trc,rc->tc', windows, conv_in, preferred_element_type=jnp.flo...  29.6 us
    all_gather x1, blocking collectives, body(): whole_filter = lax.all_gather(filt, 'dp', axis=0, tiled=True)  24.8 us
  transfers between devices with their start and end apart: 3, of which 3 were waited for; matrix products, arithmetic and copies ran while one was open for 0% of the time, Pallas kernels for 0%

commit v1 on v0

--- a/solution.py
+++ b/solution.py
@@ -2,6 +2,12 @@
 import jax.numpy as jnp
 from jax import lax
 from jax.sharding import PartitionSpec as P
+from jax.lax import all_gather
+
+
+def change_columns(vec):
+    before = all_gather(vec, axis_name="ctx").sum(axis=0)
+    return before
 
 
 def from_behind(value, axis, steps):
@@ -48,7 +54,7 @@
     grad_in = accum.astype(jnp.bfloat16)
     filt_terms = tap_rows.T
     owned = lax.psum_scatter(filt_terms, "dp", scatter_dimension=0, tiled=True)
-    grad_filt = lax.psum(owned, "ctx")
+    grad_filt = change_columns(owned)
     return (grad_in, grad_filt)
 
 

time: 698 us -> 581 us (0.83)
  waiting for transfers between devices: 344 us -> 220 us
  local copies, waits for them, and re-layouts: 169 us -> 177 us
    psum x1 -> x0, waiting for transfers between devices: 274 us -> none  [body(): grad_filt = lax.psum(owned, 'ctx')]
    all_gather x0 -> x1, waiting for transfers between devices: none -> 148 us  [change_columns(): before = all_gather(vec, axis_name='ctx').sum(axis=0)]
    gather x192, local copies, waits for them, and re-layouts: 152 us -> 159 us
where the time goes in v1:
time: 581 us; the launch traced here: 580 us
  waiting for transfers between devices  220 us (38%)
  local copies, waits for them, and re-layouts  177 us (30%)
  other arithmetic  142 us (24%)
  blocking collectives  24.6 us (4%)
  between operations  14.1 us (2%)
    gather x192, local copies, waits for them, and re-layouts  159 us
    all_gather x1, waiting for transfers between devices, change_columns(): before = all_gather(vec, axis_name='ctx').sum(axis=0)  148 us
    reduce_scatter x1, waiting for transfers between devices, body(): owned = lax.psum_scatter(filt_terms, 'dp', scatter_dimension=0, tiled=True)  70.3 us
    dot_general x8, other arithmetic, one_group(): jnp.einsum('trc,tc->rc', windows, weights, preferred_element_type=jnp.flo...  65.1 us
    add x8, other arithmetic, one_group(): accum + jnp.einsum('trc,tc->rc', windows, weights, preferred_element_type...  31.4 us
    dot_general x8, other arithmetic, one_group(): jnp.einsum('trc,rc->tc', windows, conv_in, preferred_element_type=jnp.flo...  29.6 us
    all_gather x1, blocking collectives, body(): whole_filter = lax.all_gather(filt, 'dp', axis=0, tiled=True)  24.6 us
  transfers between devices with their start and end apart: 3, of which 3 were waited for; matrix products, arithmetic and copies ran while one was open for 0% of the time, Pallas kernels for 0%

profile of v1, /device:TPU:2, one launch (start us, length us, event | category | flops | bytes accessed | tf_op | source)
XLA Modules:
  0.0 579.8 jit_solution(4671298939726447994)
XLA Ops:
  10.4 24.6 %all_gather.9 = bf16[4096,64]{0,1:T(8,128)(2,1)} all-gather(bf16[256,64]{0,1:T(8,128)(2,1)S(1)} %copy-done.3), channel_id=1, replica_groups=mesh['dp'=16,'ctx'=32] {'dp'}, dimensions={0}, use_global_device_ids=true | all-gather | bytes 557056 | tf_op jit(solution)/shard_map/all_gather | solution.py:23
  38.9 309.9 %while.23 = (s32[]{:T(128)}, f32[128,4096]{1,0:T(8,128)}, f32[64,4096]{1,0:T(8,128)}, bf16[64,4096]{1,0:T(8,128)(2,1)}, s32[128]{0:T(128)S(1)}, /*index=5*/bf16[...) while((s32[]{:T(128)}, f32[128,4096]{1,0:T(8,128)}, ...), condition=%wide.region_1.2_spmd.clone.clone, body=%wide.region_0.1_spmd.clone.sunk.clone | while | flops 34604080 | bytes 66786340 | solution.py:53
  39.7 19.9 %while.22 = (s32[]{:T(128)}, bf16[256,4096]{1,0:T(8,128)(2,1)S(1)}, s32[8,2]{0,1:T(2,128)S(1)}, bf16[8,128,4096]{2,1,0:T(8,128)(2,1)}, s32[]{:T(128)}) while((s32[]{:T(128)}, bf16[256,4096]{1,0:T(8,128)(2,1)S(1)}, s32[8,2]{0,1:T(2,128)S(1)}, bf16[8,128,4096]{2,1,0:T(8,128)(2,1)}, s32[]{:T(128)}) %tuple.56), condition=%wide.while_cond, body=%wide.while_body.sunk | while | flops 2 | bytes 2098265 | solution.py:36
  42.9 1.9 bitcast_dynamic-update-slice_fusion.5
  52.8 1.9 bitcast_dynamic-update-slice_fusion.5
  55.3 1.9 bitcast_dynamic-update-slice_fusion.5
  59.8 8.1 %multiply_reduce_fusion.6 = f32[4096,128]{0,1:T(8,128)} fusion(f32[4096,8]{0,1:T(8,128)S(1)} %bitcast_convert_fusion.6, bf16[8,128,4096]{2,1,0:T(8,128)(2,1)} %get-tuple-element.289, pred[8,128]{1,0:T(8,128)(4,1)S(1)} %broadcast_compare_fusion.3), kind=kLoop, calls=%fused_computation.4.clone.1.clone | loop fusion | flops 16252928 | bytes 10617856 | tf_op jit(solution)/shard_map/while/body/eval_jaxpr/trc,tc->rc/dot_general | solution.py:42
  67.9 3.4 bitcast_add_fusion.3
  72.7 3.7 multiply_reduce_fusion.7
  77.9 19.9 %while.22 = (s32[]{:T(128)}, bf16[256,4096]{1,0:T(8,128)(2,1)S(1)}, s32[8,2]{0,1:T(2,128)S(1)}, bf16[8,128,4096]{2,1,0:T(8,128)(2,1)}, s32[]{:T(128)}) while((s32[]{:T(128)}, bf16[256,4096]{1,0:T(8,128)(2,1)S(1)}, s32[8,2]{0,1:T(2,128)S(1)}, bf16[8,128,4096]{2,1,0:T(8,128)(2,1)}, s32[]{:T(128)}) %tuple.56), condition=%wide.while_cond, body=%wide.while_body.sunk | while | flops 2 | bytes 2098265 | solution.py:36
  81.0 1.9 bitcast_dynamic-update-slice_fusion.5
  97.9 8.1 %multiply_reduce_fusion.6 = f32[4096,128]{0,1:T(8,128)} fusion(f32[4096,8]{0,1:T(8,128)S(1)} %bitcast_convert_fusion.6, bf16[8,128,4096]{2,1,0:T(8,128)(2,1)} %get-tuple-element.289, pred[8,128]{1,0:T(8,128)(4,1)S(1)} %broadcast_compare_fusion.3), kind=kLoop, calls=%fused_computation.4.clone.1.clone | loop fusion | flops 16252928 | bytes 10617856 | tf_op jit(solution)/shard_map/while/body/eval_jaxpr/trc,tc->rc/dot_general | solution.py:42
  106.1 4.0 bitcast_add_fusion.3
  111.5 3.7 multiply_reduce_fusion.7
  116.7 19.9 %while.22 = (s32[]{:T(128)}, bf16[256,4096]{1,0:T(8,128)(2,1)S(1)}, s32[8,2]{0,1:T(2,128)S(1)}, bf16[8,128,4096]{2,1,0:T(8,128)(2,1)}, s32[]{:T(128)}) while((s32[]{:T(128)}, bf16[256,4096]{1,0:T(8,128)(2,1)S(1)}, s32[8,2]{0,1:T(2,128)S(1)}, bf16[8,128,4096]{2,1,0:T(8,128)(2,1)}, s32[]{:T(128)}) %tuple.56), condition=%wide.while_cond, body=%wide.while_body.sunk | while | flops 2 | bytes 2098265 | solution.py:36
  119.8 1.9 bitcast_dynamic-update-slice_fusion.5
  136.7 8.1 %multiply_reduce_fusion.6 = f32[4096,128]{0,1:T(8,128)} fusion(f32[4096,8]{0,1:T(8,128)S(1)} %bitcast_convert_fusion.6, bf16[8,128,4096]{2,1,0:T(8,128)(2,1)} %get-tuple-element.289, pred[8,128]{1,0:T(8,128)(4,1)S(1)} %broadcast_compare_fusion.3), kind=kLoop, calls=%fused_computation.4.clone.1.clone | loop fusion | flops 16252928 | bytes 10617856 | tf_op jit(solution)/shard_map/while/body/eval_jaxpr/trc,tc->rc/dot_general | solution.py:42
  144.9 4.0 bitcast_add_fusion.3
  150.3 3.7 multiply_reduce_fusion.7
  155.6 19.9 %while.22 = (s32[]{:T(128)}, bf16[256,4096]{1,0:T(8,128)(2,1)S(1)}, s32[8,2]{0,1:T(2,128)S(1)}, bf16[8,128,4096]{2,1,0:T(8,128)(2,1)}, s32[]{:T(128)}) while((s32[]{:T(128)}, bf16[256,4096]{1,0:T(8,128)(2,1)S(1)}, s32[8,2]{0,1:T(2,128)S(1)}, bf16[8,128,4096]{2,1,0:T(8,128)(2,1)}, s32[]{:T(128)}) %tuple.56), condition=%wide.while_cond, body=%wide.while_body.sunk | while | flops 2 | bytes 2098265 | solution.py:36
  158.7 1.9 bitcast_dynamic-update-slice_fusion.5
  175.6 8.1 %multiply_reduce_fusion.6 = f32[4096,128]{0,1:T(8,128)} fusion(f32[4096,8]{0,1:T(8,128)S(1)} %bitcast_convert_fusion.6, bf16[8,128,4096]{2,1,0:T(8,128)(2,1)} %get-tuple-element.289, pred[8,128]{1,0:T(8,128)(4,1)S(1)} %broadcast_compare_fusion.3), kind=kLoop, calls=%fused_computation.4.clone.1.clone | loop fusion | flops 16252928 | bytes 10617856 | tf_op jit(solution)/shard_map/while/body/eval_jaxpr/trc,tc->rc/dot_general | solution.py:42
  183.7 4.0 bitcast_add_fusion.3
  189.1 3.7 multiply_reduce_fusion.7
  194.4 19.9 %while.22 = (s32[]{:T(128)}, bf16[256,4096]{1,0:T(8,128)(2,1)S(1)}, s32[8,2]{0,1:T(2,128)S(1)}, bf16[8,128,4096]{2,1,0:T(8,128)(2,1)}, s32[]{:T(128)}) while((s32[]{:T(128)}, bf16[256,4096]{1,0:T(8,128)(2,1)S(1)}, s32[8,2]{0,1:T(2,128)S(1)}, bf16[8,128,4096]{2,1,0:T(8,128)(2,1)}, s32[]{:T(128)}) %tuple.56), condition=%wide.while_cond, body=%wide.while_body.sunk | while | flops 2 | bytes 2098265 | solution.py:36
  197.5 1.9 bitcast_dynamic-update-slice_fusion.5
  214.4 8.1 %multiply_reduce_fusion.6 = f32[4096,128]{0,1:T(8,128)} fusion(f32[4096,8]{0,1:T(8,128)S(1)} %bitcast_convert_fusion.6, bf16[8,128,4096]{2,1,0:T(8,128)(2,1)} %get-tuple-element.289, pred[8,128]{1,0:T(8,128)(4,1)S(1)} %broadcast_compare_fusion.3), kind=kLoop, calls=%fused_computation.4.clone.1.clone | loop fusion | flops 16252928 | bytes 10617856 | tf_op jit(solution)/shard_map/while/body/eval_jaxpr/trc,tc->rc/dot_general | solution.py:42
  222.5 4.0 bitcast_add_fusion.3
  227.9 3.7 multiply_reduce_fusion.7
  233.2 19.9 %while.22 = (s32[]{:T(128)}, bf16[256,4096]{1,0:T(8,128)(2,1)S(1)}, s32[8,2]{0,1:T(2,128)S(1)}, bf16[8,128,4096]{2,1,0:T(8,128)(2,1)}, s32[]{:T(128)}) while((s32[]{:T(128)}, bf16[256,4096]{1,0:T(8,128)(2,1)S(1)}, s32[8,2]{0,1:T(2,128)S(1)}, bf16[8,128,4096]{2,1,0:T(8,128)(2,1)}, s32[]{:T(128)}) %tuple.56), condition=%wide.while_cond, body=%wide.while_body.sunk | while | flops 2 | bytes 2098265 | solution.py:36
  236.3 1.9 bitcast_dynamic-update-slice_fusion.5
  253.2 8.1 %multiply_reduce_fusion.6 = f32[4096,128]{0,1:T(8,128)} fusion(f32[4096,8]{0,1:T(8,128)S(1)} %bitcast_convert_fusion.6, bf16[8,128,4096]{2,1,0:T(8,128)(2,1)} %get-tuple-element.289, pred[8,128]{1,0:T(8,128)(4,1)S(1)} %broadcast_compare_fusion.3), kind=kLoop, calls=%fused_computation.4.clone.1.clone | loop fusion | flops 16252928 | bytes 10617856 | tf_op jit(solution)/shard_map/while/body/eval_jaxpr/trc,tc->rc/dot_general | solution.py:42
  261.3 4.0 bitcast_add_fusion.3
  266.7 3.7 multiply_reduce_fusion.7
  272.0 19.9 %while.22 = (s32[]{:T(128)}, bf16[256,4096]{1,0:T(8,128)(2,1)S(1)}, s32[8,2]{0,1:T(2,128)S(1)}, bf16[8,128,4096]{2,1,0:T(8,128)(2,1)}, s32[]{:T(128)}) while((s32[]{:T(128)}, bf16[256,4096]{1,0:T(8,128)(2,1)S(1)}, s32[8,2]{0,1:T(2,128)S(1)}, bf16[8,128,4096]{2,1,0:T(8,128)(2,1)}, s32[]{:T(128)}) %tuple.56), condition=%wide.while_cond, body=%wide.while_body.sunk | while | flops 2 | bytes 2098265 | solution.py:36
  275.1 1.9 bitcast_dynamic-update-slice_fusion.5
  292.0 8.1 %multiply_reduce_fusion.6 = f32[4096,128]{0,1:T(8,128)} fusion(f32[4096,8]{0,1:T(8,128)S(1)} %bitcast_convert_fusion.6, bf16[8,128,4096]{2,1,0:T(8,128)(2,1)} %get-tuple-element.289, pred[8,128]{1,0:T(8,128)(4,1)S(1)} %broadcast_compare_fusion.3), kind=kLoop, calls=%fused_computation.4.clone.1.clone | loop fusion | flops 16252928 | bytes 10617856 | tf_op jit(solution)/shard_map/while/body/eval_jaxpr/trc,tc->rc/dot_general | solution.py:42
  300.1 4.0 bitcast_add_fusion.3
  305.5 3.7 multiply_reduce_fusion.7
  310.8 19.9 %while.22 = (s32[]{:T(128)}, bf16[256,4096]{1,0:T(8,128)(2,1)S(1)}, s32[8,2]{0,1:T(2,128)S(1)}, bf16[8,128,4096]{2,1,0:T(8,128)(2,1)}, s32[]{:T(128)}) while((s32[]{:T(128)}, bf16[256,4096]{1,0:T(8,128)(2,1)S(1)}, s32[8,2]{0,1:T(2,128)S(1)}, bf16[8,128,4096]{2,1,0:T(8,128)(2,1)}, s32[]{:T(128)}) %tuple.56), condition=%wide.while_cond, body=%wide.while_body.sunk | while | flops 2 | bytes 2098265 | solution.py:36
  313.9 1.9 bitcast_dynamic-update-slice_fusion.5
  330.8 8.1 %multiply_reduce_fusion.6 = f32[4096,128]{0,1:T(8,128)} fusion(f32[4096,8]{0,1:T(8,128)S(1)} %bitcast_convert_fusion.6, bf16[8,128,4096]{2,1,0:T(8,128)(2,1)} %get-tuple-element.289, pred[8,128]{1,0:T(8,128)(4,1)S(1)} %broadcast_compare_fusion.3), kind=kLoop, calls=%fused_computation.4.clone.1.clone | loop fusion | flops 16252928 | bytes 10617856 | tf_op jit(solution)/shard_map/while/body/eval_jaxpr/trc,tc->rc/dot_general | solution.py:42
  339.0 4.0 bitcast_add_fusion.3
  344.4 3.7 multiply_reduce_fusion.7
  348.8 70.3 %reduce-scatter.2.cloned.1.call-done = f32[256,64]{0,1:T(8,128)} async-done(((f32[4096,64]{0,1:T(8,128)}), f32[256,64]{0,1:T(8,128)}) %reduce-scatter.2.cloned.1.call-update) | async-done | bytes 65552 | tf_op jit(solution)/shard_map/reduce_scatter | solution.py:56
  419.1 2.7 convert_element_type.15
  421.8 148.1 %all-gather.3.cloned.1.call-done = f32[8192,64]{0,1:T(8,128)} async-done(((f32[256,64]{0,1:T(8,128)}), f32[8192,64]{0,1:T(8,128)}) %all-gather.3.cloned.1.call-update) | async-done | bytes 2097168 | tf_op jit(solution)/shard_map/all_gather | solution.py:9
  569.9 2.2 copy.23
  (282 shorter events, 172.2 us)
Async XLA Ops:
  7.2 3.2 copy-start.4
  7.2 3.2 copy-start.3
  7.2 411.9 %reduce-scatter.2.cloned.1.call-start = ((), (), s32[]{:S(2)}) async-start(), calls=%async_computation.1 | async-start | bytes 1114112 | tf_op jit(solution)/shard_map/reduce_scatter | solution.py:56
  9.0 26.0 %copy-start.2 = (bf16[128,4096]{1,0:T(8,128)(2,1)}, bf16[128,4096]{1,0:T(8,128)(2,1)S(1)}, u32[]{:S(2)}) copy-start(bf16[128,4096]{1,0:T(8,128)(2,1)S(1)} %multiply_convert_fusion) | copy-start | bytes 3145732
  9.0 27.1 %collective-permute-start = (bf16[128,4096]{1,0:T(8,128)(2,1)S(1)}, bf16[128,4096]{1,0:T(8,128)(2,1)}, u32[]{:S(2)}, u32[]{:S(2)}) collective-permute-start(bf16[128,4096]{1,0:T(8,128)(2,1)S(1)} %multiply_convert_fusion), channel_id=1, source_target_pairs={{1,0},{2,1},{3,2},{4,3},{5,4},{6,5},{7,6},{8,7},{9,8},{10,9},{11,1... | collective-permute-start | bytes 3145736 | tf_op jit(solution)/shard_map/ppermute | solution.py:16
  35.0 3.8 copy-start.1
  67.9 4.8 copy-start
  106.1 5.4 copy-start
  144.9 5.4 copy-start
  183.7 5.4 copy-start
  222.5 5.4 copy-start
  261.3 5.4 copy-start
  300.1 5.4 copy-start
  339.0 5.4 copy-start
  348.8 221.2 %all-gather.3.cloned.1.call-start = ((), (), s32[]{:S(2)}) async-start(), calls=%async_computation.2 | async-start | bytes 2162688 | tf_op jit(solution)/shard_map/all_gather | solution.py:9
Sparse Core Ops, SparseCore 0:
  348.9 70.1 reduce-scatter.1
  422.0 147.8 all-gather.2
